TPU v7x, 256 devices: a whole 4x4x8 slice. The times are simulated.
256 devices in a mesh: dp: 16 (over x_lo, z), fsdp: 16 (over y, x_hi, core).
Axes of the slice: x: 4 (x_hi: 2, x_lo: 2; x = x_hi * 2 + x_lo), y: 4, z: 8, core: 2. Of those that a mesh axis runs over, the one named last changes fastest.
Arguments:
- hidden_states: bfloat16 [32768, 8192], P(('dp', 'fsdp')), may hold values from -450 to 450
- gain: float32 [8192], replicated, may hold values from 0.1 to 1.9
- key_weight: bfloat16 [8192, 512], P('fsdp'), may hold values from -0.0625 to 0.0625
- key_cotangent: bfloat16 [32768, 512], P(('dp', 'fsdp')), may hold values from -18 to 18
- bucket: int32 [5, 32768], P(None, 'fsdp'), may hold values from 0 to 255
- sign_bits: int32 [5, 32768], P(None, 'fsdp'), may hold values from 0 to 1
- momentum: float32 [16, 5, 32768], P('fsdp', None, 'dp'), may hold values from -12 to 12
- error: float32 [16, 5, 32768], P('fsdp', None, 'dp'), may hold values from -12 to 12
Outputs:
- hidden_grad: bfloat16 [32768, 8192], P(('dp', 'fsdp'))
- momentum_new: float32 [16, 5, 32768], P('fsdp', None, 'dp')
- error_new: float32 [16, 5, 32768], P('fsdp', None, 'dp')
- update: float32 [8192, 512], P('fsdp')
All inputs are finite; a program needn't handle non-finite values.
Results may differ from a plain program's by a relative error of at most 0.0095.
Values may be sent and summed in bfloat16 or wider, within the bound.
A program may use at most 128 MiB of HBM per device.

v0:
```python
import math
import jax
import jax.numpy as jnp
from jax import lax
from jax.sharding import PartitionSpec as P

ROWS = 5
NBB = 256
BLOCK = 128
EPS = 1e-05
DECAY = 0.9
THRESHOLD = 1.0


def normalize(states, gain):
    values = states.astype(jnp.float32)
    inverse_rms = lax.rsqrt(jnp.mean(values * values, axis=1, keepdims=True) + EPS)
    normed = values * inverse_rms
    return (normed, inverse_rms, (normed * gain).astype(jnp.bfloat16))


def norm_backward(input_grad, gain, normed, inverse_rms):
    scaled = input_grad.astype(jnp.float32) * gain
    mean_term = jnp.mean(scaled * normed, axis=1, keepdims=True)
    return (inverse_rms * (scaled - normed * mean_term)).astype(jnp.bfloat16)


def split_product(selector, values, numbers):
    upper = values.astype(jnp.bfloat16)
    lower = (values - upper.astype(jnp.float32)).astype(jnp.bfloat16)
    first = lax.dot_general(selector, upper, numbers, preferred_element_type=jnp.float32)
    return first + lax.dot_general(selector, lower, numbers, preferred_element_type=jnp.float32)


def middle_three(first, second, third):
    return jnp.maximum(jnp.minimum(first, second), jnp.minimum(jnp.maximum(first, second), third))


def middle_five(items):
    upper_pair = jnp.minimum(jnp.maximum(items[0], items[1]), jnp.maximum(items[2], items[3]))
    lower_pair = jnp.maximum(jnp.minimum(items[0], items[1]), jnp.minimum(items[2], items[3]))
    return middle_three(items[4], upper_pair, lower_pair)


def on_device(hidden_states, gain, key_weight, key_cotangent, bucket, sign_bits, momentum, error):
    normed, inverse_rms, inputs = normalize(hidden_states, gain)
    fsdp_count = lax.axis_size("fsdp")
    dp_count = lax.axis_size("dp")
    local_rows = key_weight.shape[0]
    grad_scale = 1.0 / math.sqrt(inputs.shape[0] * fsdp_count)
    contract_last = (((1,), (1,)), ((), ()))
    contract_first = (((0,), (0,)), ((), ()))
    contract_plain = (((1,), (0,)), ((), ()))
    input_grad = lax.dot_general(
        key_cotangent,
        lax.all_gather(key_weight, "fsdp", axis=0, tiled=True),
        contract_last,
        preferred_element_type=jnp.float32,
    ).astype(jnp.bfloat16)
    weight_grad = lax.psum_scatter(
        lax.dot_general(inputs, key_cotangent, contract_first, preferred_element_type=jnp.float32),
        "fsdp",
        scatter_dimension=0,
        tiled=True,
    )
    hidden_grad = norm_backward(input_grad, gain, normed, inverse_rms)
    blocks = (weight_grad * grad_scale).reshape(-1, BLOCK)
    signs = (2 * sign_bits - 1).astype(jnp.bfloat16)
    sign_values = (2 * sign_bits - 1).astype(jnp.float32)
    zero_sel = jnp.zeros((), jnp.bfloat16)
    bucket_ids = lax.broadcasted_iota(jnp.int32, (NBB, 1), 0)
    local_table = jnp.stack(
        [
            split_product(
                jnp.where(
                    bucket[row_index][None, :] == bucket_ids, signs[row_index][None, :], zero_sel
                ),
                blocks,
                contract_plain,
            )
            for row_index in range(ROWS)
        ]
    ).reshape(1, ROWS, NBB * BLOCK)
    share = momentum.shape[2]
    offset = lax.axis_index("dp") * share
    total = lax.psum(local_table, "dp")
    momentum_all, error_all = (
        lax.all_gather(momentum, "dp", axis=2, tiled=True),
        lax.all_gather(error, "dp", axis=2, tiled=True),
    )
    momentum_all = DECAY * momentum_all + total / dp_count
    error_all = error_all + momentum_all
    momentum_new = lax.dynamic_slice_in_dim(momentum_all, offset, share, 2)
    error_mid = lax.dynamic_slice_in_dim(error_all, offset, share, 2)
    error_rows = error_all.reshape(ROWS, NBB, BLOCK)
    reads = [
        error_rows[row_index][bucket[row_index]] * sign_values[row_index][:, None]
        for row_index in range(ROWS)
    ]
    estimate = middle_five(reads)
    update = estimate - jnp.clip(estimate, -THRESHOLD, THRESHOLD)
    share_buckets = share // BLOCK
    share_ids = bucket_ids[:share_buckets] + lax.axis_index("dp") * share_buckets
    sketched = jnp.stack(
        [
            split_product(
                jnp.where(
                    bucket[row_index][None, :] == share_ids, signs[row_index][None, :], zero_sel
                ),
                update,
                contract_plain,
            )
            for row_index in range(ROWS)
        ]
    ).reshape(1, ROWS, share)
    error_new = error_mid - sketched
    return (hidden_grad, momentum_new, error_new, update.reshape(local_rows, -1))


def solution(mesh):
    in_specs = (
        P(("dp", "fsdp"), None),
        P(),
        P("fsdp", None),
        P(("dp", "fsdp"), None),
        P(None, "fsdp"),
        P(None, "fsdp"),
        P("fsdp", None, "dp"),
        P("fsdp", None, "dp"),
    )
    out_specs = (
        P(("dp", "fsdp"), None),
        P("fsdp", None, "dp"),
        P("fsdp", None, "dp"),
        P("fsdp", None),
    )
    return jax.shard_map(
        on_device, mesh=mesh, in_specs=in_specs, out_specs=out_specs, check_vma=False
    )
```

profile of v0, /device:TPU:8, one launch (start us, length us, event | category | flops | bytes accessed | tf_op | source)
XLA Modules:
  0.0 459.5 jit_solution(4730571802656826122)
XLA Ops:
  8.0 2.1 fusion.10
  10.1 8.2 %fusion.11 = f32[8192,512]{1,0:T(8,128)} fusion(bf16[128,512]{1,0:T(8,128)(2,1)S(1)} %copy-done, bf16[128,8192]{1,0:T(8,128)(2,1)S(1)} %copy-done.1, f32[8192]{0:T(1024)S(1)} %copy-done.18, f32[128]{0:T(128)S(1)} %add_rsqrt_fusion), kind=kOutput, calls=%fused_computation.19 | convolution fusion | flops 1077936128 | bytes 19038720 | tf_op jit(solution)/shard_map/dot_general | solution.py:61
  28.5 42.3 %all_gather.10 = f32[1,5,32768]{2,0,1:T(1,128)} all-gather(f32[1,5,2048]{2,0,1:T(1,128)S(1)} %copy-done.28), channel_id=1, replica_groups=mesh['dp'=16,'fsdp'=16] {'dp'}, dimensions={2}, use_global_device_ids=true | all-gather | bytes 696320 | tf_op jit(solution)/shard_map/all_gather | solution.py:88
  70.8 36.0 %all_gather.11 = f32[1,5,32768]{2,0,1:T(1,128)} all-gather(f32[1,5,2048]{2,0,1:T(1,128)S(1)} %copy-done.29), channel_id=1, replica_groups=mesh['dp'=16,'fsdp'=16] {'dp'}, dimensions={2}, use_global_device_ids=true | all-gather | bytes 696320 | tf_op jit(solution)/shard_map/all_gather | solution.py:89
  106.9 9.1 %fusion.5 = (f32[128]{0:T(128)S(1)}, f32[128,8192]{1,0:T(8,128)}) fusion(bf16[128,8192]{1,0:T(8,128)(2,1)S(1)} %copy-done.1, f32[128]{0:T(128)S(1)} %add_rsqrt_fusion, f32[8192]{0:T(1024)S(1)} %copy-done.18, bf16[128,512]{1,0:T(8,128)(2,1)S(1)} %copy-done, bf16[8192,512]{1,0:T(8,128)(2,1)} %all-gather.2.cloned.1.call-done), kind=kOutput, calls=%fused_computation.13 | convolution fusion | flops 1081081728 | bytes 14844928 | tf_op jit(solution)/shard_map/dot_general | solution.py:54
  116.5 133.0 %reduce-scatter.2.cloned.1.call-done = f32[512,512]{1,0:T(8,128)} async-done(((f32[8192,512]{1,0:T(8,128)}), f32[512,512]{1,0:T(8,128)}) %reduce-scatter.2.cloned.1.call-update) | async-done | bytes 1048592 | tf_op jit(solution)/shard_map/reduce_scatter | solution.py:60
  249.6 2.3 broadcast_multiply_fusion
  251.9 1.3 reshape.223
  258.7 4.5 fusion.8
  263.2 131.6 %all-reduce.2.cloned.1.call-done = f32[1,5,32768]{2,0,1:T(1,128)} async-done(((f32[1,5,32768]{2,0,1:T(1,128)}), f32[1,5,32768]{2,0,1:T(1,128)}) %all-reduce.2.cloned.1.call-update) | async-done | bytes 655376 | tf_op jit(solution)/shard_map/psum | solution.py:86
  394.7 3.5 fusion.153
  398.3 5.7 %gather_fusion = f32[2048,128]{1,0:T(8,128)S(1)} fusion(f32[256,128]{1,0:T(8,128)S(1)} %bitcast.114, s32[2048]{0:T(1024)S(1)} %copy-done.48), kind=kCustom, calls=%fused_computation | custom fusion | bytes 2105344 | tf_op jit(solution)/shard_map/gather | solution.py:97
  404.0 1.2 gather.30
  405.2 5.5 %gather_fusion.1 = f32[2048,128]{1,0:T(8,128)S(1)} fusion(f32[256,128]{1,0:T(8,128)S(1)} %bitcast.113, s32[2048]{0:T(1024)S(1)} %copy-done.47), kind=kCustom, calls=%fused_computation.1 | custom fusion | bytes 2105344 | tf_op jit(solution)/shard_map/gather | solution.py:97
  410.7 1.1 gather.31
  411.8 7.6 %gather_fusion.2 = f32[2048,128]{1,0:T(8,128)} fusion(f32[256,128]{1,0:T(8,128)S(1)} %bitcast.112, s32[2048]{0:T(1024)S(1)} %copy-done.46), kind=kCustom, calls=%fused_computation.2 | custom fusion | bytes 2105344 | tf_op jit(solution)/shard_map/gather | solution.py:97
  419.4 2.4 gather.32
  421.8 6.4 %gather_fusion.3 = f32[2048,128]{1,0:T(8,128)S(1)} fusion(f32[256,128]{1,0:T(8,128)S(1)} %bitcast.111, s32[2048]{0:T(1024)} %broadcast_clamp_fusion.1), kind=kCustom, calls=%fused_computation.3 | custom fusion | bytes 2105344 | tf_op jit(solution)/shard_map/gather | solution.py:97
  428.2 1.3 gather.33
  429.5 7.6 %gather_fusion.4 = f32[2048,128]{1,0:T(8,128)} fusion(f32[256,128]{1,0:T(8,128)S(1)} %bitcast.110, s32[2048]{0:T(1024)S(1)} %copy-done.45), kind=kCustom, calls=%fused_computation.4 | custom fusion | bytes 2105344 | tf_op jit(solution)/shard_map/gather | solution.py:97
  437.2 2.5 gather.34
  439.8 3.5 subtract_convert_fusion
  445.9 1.5 dynamic-slice_subtract_fusion
  450.7 2.3 clamp_subtract_fusion
  (162 shorter events, 22.5 us)
Async XLA Ops:
  7.2 99.7 %all-gather.2.cloned.1.call-start = ((), (), s32[]{:S(2)}) async-start(), calls=%async_computation.1 | async-start | bytes 8912896 | tf_op jit(solution)/shard_map/all_gather | solution.py:56
  7.9 241.6 %reduce-scatter.2.cloned.1.call-start = ((), (), s32[]{:S(2)}) async-start(), calls=%async_computation.2 | async-start | bytes 17825792 | tf_op jit(solution)/shard_map/reduce_scatter | solution.py:60
  10.1 96.8 %copy-start.49 = (f32[128]{0:T(128)}, f32[128]{0:T(128)S(1)}, u32[]{:S(2)}) copy-start(f32[128]{0:T(128)S(1)} %add_rsqrt_fusion) | copy-start | bytes 1540
  18.3 7.1 %copy-start.19 = (s32[5,2048]{1,0:T(8,128)S(1)}, s32[5,2048]{1,0:T(8,128)}, u32[]{:S(2)}) copy-start(s32[5,2048]{1,0:T(8,128)} %param.12) | copy-start | bytes 122884
  18.3 10.2 %copy-start.28 = (f32[1,5,2048]{2,0,1:T(1,128)S(1)}, f32[1,5,2048]{2,0,1:T(1,128)}, u32[]{:S(2)}) copy-start(f32[1,5,2048]{2,0,1:T(1,128)} %param.14) | copy-start | bytes 122884
  18.3 52.5 %copy-start.29 = (f32[1,5,2048]{2,0,1:T(1,128)S(1)}, f32[1,5,2048]{2,0,1:T(1,128)}, u32[]{:S(2)}) copy-start(f32[1,5,2048]{2,0,1:T(1,128)} %param.15) | copy-start | bytes 122884
  18.3 376.4 %all-reduce.2.cloned.1.call-start = ((), (), s32[]{:S(2)}) async-start(), calls=%async_computation.3 | async-start | bytes 1310720 | tf_op jit(solution)/shard_map/psum | solution.py:86
  25.4 228.4 %copy-start.32 = (bf16[2048]{0:T(1024)(128)(2,1)}, bf16[2048]{0:T(1024)(128)(2,1)S(1)}, u32[]{:S(2)}) copy-start(bf16[2048]{0:T(1024)(128)(2,1)S(1)} %get-tuple-element.12) | copy-start | bytes 12292
  25.4 229.2 %copy-start.30 = (bf16[2048]{0:T(1024)(128)(2,1)}, bf16[2048]{0:T(1024)(128)(2,1)S(1)}, u32[]{:S(2)}) copy-start(bf16[2048]{0:T(1024)(128)(2,1)S(1)} %get-tuple-element.13) | copy-start | bytes 12292
  25.4 230.1 %copy-start.34 = (bf16[2048]{0:T(1024)(128)(2,1)}, bf16[2048]{0:T(1024)(128)(2,1)S(1)}, u32[]{:S(2)}) copy-start(bf16[2048]{0:T(1024)(128)(2,1)S(1)} %get-tuple-element.11) | copy-start | bytes 12292
  25.4 231.0 %copy-start.36 = (bf16[2048]{0:T(1024)(128)(2,1)}, bf16[2048]{0:T(1024)(128)(2,1)S(1)}, u32[]{:S(2)}) copy-start(bf16[2048]{0:T(1024)(128)(2,1)S(1)} %get-tuple-element.10) | copy-start | bytes 12292
  25.4 231.8 %copy-start.38 = (bf16[2048]{0:T(1024)(128)(2,1)}, bf16[2048]{0:T(1024)(128)(2,1)S(1)}, u32[]{:S(2)}) copy-start(bf16[2048]{0:T(1024)(128)(2,1)S(1)} %get-tuple-element.9) | copy-start | bytes 12292
  106.8 148.7 %copy-start.20 = (s32[1,2048]{1,0:T(1,128)}, s32[1,2048]{1,0:T(1,128)S(1)}, u32[]{:S(2)}) copy-start(s32[1,2048]{1,0:T(1,128)S(1)} %get-tuple-element.38) | copy-start | bytes 24580
  106.8 149.6 %copy-start.22 = (s32[1,2048]{1,0:T(1,128)}, s32[1,2048]{1,0:T(1,128)S(1)}, u32[]{:S(2)}) copy-start(s32[1,2048]{1,0:T(1,128)S(1)} %get-tuple-element.41) | copy-start | bytes 24580
  106.8 150.4 %copy-start.24 = (s32[1,2048]{1,0:T(1,128)}, s32[1,2048]{1,0:T(1,128)S(1)}, u32[]{:S(2)}) copy-start(s32[1,2048]{1,0:T(1,128)S(1)} %get-tuple-element.37) | copy-start | bytes 24580
  258.7 136.1 %copy-start.10 = (f32[1,5,32768]{2,0,1:T(1,128)S(1)}, f32[1,5,32768]{2,0,1:T(1,128)}, u32[]{:S(2)}) copy-start(f32[1,5,32768]{2,0,1:T(1,128)} %all_gather.10) | copy-start | bytes 1966084
  258.7 136.1 %copy-start.11 = (f32[1,5,32768]{2,0,1:T(1,128)S(1)}, f32[1,5,32768]{2,0,1:T(1,128)}, u32[]{:S(2)}) copy-start(f32[1,5,32768]{2,0,1:T(1,128)} %all_gather.11) | copy-start | bytes 1966084
  263.2 135.1 %copy-start.48 = (s32[2048]{0:T(1024)S(1)}, s32[2048]{0:T(1024)}, u32[]{:S(2)}) copy-start(s32[2048]{0:T(1024)} %broadcast_clamp_fusion.4) | copy-start | bytes 24580
  398.2 5.8 %copy-start.9 = (f32[1,5,32768]{2,0,1:T(1,128)}, f32[1,5,32768]{2,0,1:T(1,128)S(1)}, u32[]{:S(2)}) copy-start(f32[1,5,32768]{2,0,1:T(1,128)S(1)} %get-tuple-element.16) | copy-start | bytes 1966084
  439.7 3.8 copy-start.23
  439.7 3.8 copy-start.37
  439.8 4.1 copy-start.21
  439.8 4.1 copy-start.35
  439.8 4.3 copy-start.33
  (29 other events, 69.0 us)
Sparse Core Ops, SparseCore 0:
  10.8 85.1 all-gather.1
  100.5 148.9 reduce-scatter.1
  258.8 135.9 all-reduce.1
where the time goes:
time: 460 us; the launch traced here: 459 us
  waiting for transfers between devices  265 us (58%)
  blocking collectives  78.3 us (17%)
  local copies, waits for them, and re-layouts  53.3 us (12%)
  matrix products  24 us (5%)
  other arithmetic  23.9 us (5%)
  between operations  14.5 us (3%)
    reduce_scatter x1, waiting for transfers between devices, on_device(): lax.psum_scatter(lax.dot_general(inputs, key_cotangent, contract_first, p...  133 us
    psum x1, waiting for transfers between devices, on_device(): total = lax.psum(local_table, 'dp')  132 us
    all_gather x1, blocking collectives, on_device(): lax.all_gather(momentum, 'dp', axis=2, tiled=True)  42.3 us
    gather x10, local copies, waits for them, and re-layouts, on_device(): error_rows[row_index][bucket[row_index]] * sign_values[row_index][:, None]  41.2 us
    all_gather x1, blocking collectives, on_device(): lax.all_gather(error, 'dp', axis=2, tiled=True)  36 us
  transfers between devices with their start and end apart: 3, of which 2 were waited for; matrix products, arithmetic and copies ran while one was open for 7% of the time, Pallas kernels for 0%

commit v1 on v0

--- a/solution.py
+++ b/solution.py
@@ -83,7 +83,8 @@
     ).reshape(1, ROWS, NBB * BLOCK)
     share = momentum.shape[2]
     offset = lax.axis_index("dp") * share
-    total = lax.psum(local_table, "dp")
+    terms = lax.all_gather(local_table, "dp")
+    total = jnp.sum(terms, axis=0)
     momentum_all, error_all = (
         lax.all_gather(momentum, "dp", axis=2, tiled=True),
         lax.all_gather(error, "dp", axis=2, tiled=True),

time: 460 us -> 454 us (0.987)
    psum x1 -> x0, waiting for transfers between devices: 132 us -> none  [on_device(): total = lax.psum(local_table, 'dp')]
    all_gather x0 -> x1, waiting for transfers between devices: none -> 106 us  [on_device(): terms = lax.all_gather(local_table, 'dp')]
    reduce_scatter x1, waiting for transfers between devices: 133 us -> 156 us  [on_device(): lax.psum_scatter(lax.dot_general(inputs, key_cotangent, contract_first, p...]
    reduce_sum x0 -> x1, other arithmetic: none -> 8.41 us  [on_device(): total = jnp.sum(terms, axis=0)]
  transfers between devices with their start and end apart: 3 -> 3, of which waited for: 2 -> 2; matrix products, arithmetic and copies ran while one was open for 7% -> 5% of each run, Pallas kernels for 0% -> 0%
where the time goes in v1:
time: 454 us; the launch traced here: 452 us
  waiting for transfers between devices  262 us (58%)
  blocking collectives  74.9 us (16%)
  local copies, waits for them, and re-layouts  51.5 us (11%)
  other arithmetic  26.6 us (6%)
  matrix products  22.7 us (5%)
  between operations  14.5 us (3%)
    reduce_scatter x1, waiting for transfers between devices, on_device(): lax.psum_scatter(lax.dot_general(inputs, key_cotangent, contract_first, p...  156 us
    all_gather x1, waiting for transfers between devices, on_device(): terms = lax.all_gather(local_table, 'dp')  106 us
    gather x10, local copies, waits for them, and re-layouts, on_device(): error_rows[row_index][bucket[row_index]] * sign_values[row_index][:, None]  41.6 us
    all_gather x1, blocking collectives, on_device(): lax.all_gather(momentum, 'dp', axis=2, tiled=True)  39.1 us
    all_gather x1, blocking collectives, on_device(): lax.all_gather(error, 'dp', axis=2, tiled=True)  35.8 us
    dot_general x1, matrix products, on_device(): lax.dot_general(inputs, key_cotangent, contract_first, preferred_element_...  9.78 us
  transfers between devices with their start and end apart: 3, of which 2 were waited for; matrix products, arithmetic and copies ran while one was open for 5% of the time, Pallas kernels for 0%

profile of v1, /device:TPU:8, one launch (start us, length us, event | category | flops | bytes accessed | tf_op | source)
XLA Modules:
  0.0 452.4 jit_solution(17887697035218379490)
XLA Ops:
  7.2 2.1 fusion.10
  9.4 9.8 %fusion.11 = f32[8192,512]{1,0:T(8,128)} fusion(bf16[128,512]{1,0:T(8,128)(2,1)S(1)} %copy-done, bf16[128,8192]{1,0:T(8,128)(2,1)} %param.8, f32[8192]{0:T(1024)} %param.9, f32[128]{0:T(128)S(1)} %add_rsqrt_fusion), kind=kOutput, calls=%fused_computation.19 | convolution fusion | flops 1077936128 | bytes 19038720 | tf_op jit(solution)/shard_map/dot_general | solution.py:61
  20.2 155.5 %reduce-scatter.2.cloned.1.call-done = f32[512,512]{1,0:T(8,128)} async-done(((f32[8192,512]{1,0:T(8,128)}), f32[512,512]{1,0:T(8,128)}) %reduce-scatter.2.cloned.1.call-update) | async-done | bytes 1048592 | tf_op jit(solution)/shard_map/reduce_scatter | solution.py:60
  175.8 1.3 broadcast_multiply_fusion.1
  190.6 39.1 %all_gather.13 = f32[1,5,32768]{2,0,1:T(1,128)} all-gather(f32[1,5,2048]{2,0,1:T(1,128)S(1)} %copy-done.27), channel_id=1, replica_groups=mesh['dp'=16,'fsdp'=16] {'dp'}, dimensions={2}, use_global_device_ids=true | all-gather | bytes 696320 | tf_op jit(solution)/shard_map/all_gather | solution.py:89
  229.7 35.8 %all_gather.15 = f32[1,5,32768]{2,0,1:T(1,128)} all-gather(f32[1,5,2048]{2,0,1:T(1,128)S(1)} %copy-done.28), channel_id=1, replica_groups=mesh['dp'=16,'fsdp'=16] {'dp'}, dimensions={2}, use_global_device_ids=true | all-gather | bytes 696320 | tf_op jit(solution)/shard_map/all_gather | solution.py:90
  265.6 6.3 %fusion.5 = (f32[128]{0:T(128)S(1)}, f32[128,8192]{1,0:T(8,128)S(1)}) fusion(bf16[128,8192]{1,0:T(8,128)(2,1)S(1)} %copy-done.2, f32[128]{0:T(128)S(1)} %add_rsqrt_fusion, f32[8192]{0:T(1024)S(1)} %copy-done.17, bf16[128,512]{1,0:T(8,128)(2,1)S(1)} %copy-done, bf16[8192,512]{1,0:T(8,128)(2,1)} %all-gather.3.cloned.1.call-done), kind=kOutput, calls=%fused_computation.13 | convolution fusion | flops 1081081728 | bytes 14844928 | tf_op jit(solution)/shard_map/dot_general | solution.py:54
  271.9 2.3 fusion.8
  274.1 105.8 %all-gather.5.cloned.1.call-done = f32[16,1,5,32768]{3,1,2,0:T(1,128)} async-done(((f32[1,1,5,32768]{3,1,2,0:T(1,128)}), f32[16,1,5,32768]{3,1,2,0:T(1,128)}) %all-gather.5.cloned.1.call-update) | async-done | bytes 10485776 | tf_op jit(solution)/shard_map/all_gather | solution.py:86
  379.9 8.4 %reduce_sum.29 = f32[5,32768]{1,0:T(8,128)S(1)} reduce(f32[16,1,5,32768]{3,1,2,0:T(1,128)} %all-gather.5.cloned.1.call-done, f32[]{:T(128)} %constant.6.clone.1), dimensions={0,1}, to_apply=%region_3.4 | reduce | flops 2457600 | bytes 11141124 | tf_op jit(solution)/shard_map/reduce_sum | solution.py:87
  388.5 2.2 fusion.153
  390.7 5.5 %gather_fusion = f32[2048,128]{1,0:T(8,128)S(1)} fusion(f32[256,128]{1,0:T(8,128)S(1)} %bitcast.114, s32[2048]{0:T(1024)S(1)} %broadcast_clamp_fusion.4), kind=kCustom, calls=%fused_computation | custom fusion | bytes 2105344 | tf_op jit(solution)/shard_map/gather | solution.py:98
  396.2 1.2 gather.30
  397.4 5.5 %gather_fusion.1 = f32[2048,128]{1,0:T(8,128)S(1)} fusion(f32[256,128]{1,0:T(8,128)S(1)} %bitcast.113, s32[2048]{0:T(1024)S(1)} %broadcast_clamp_fusion.3), kind=kCustom, calls=%fused_computation.1 | custom fusion | bytes 2105344 | tf_op jit(solution)/shard_map/gather | solution.py:98
  402.8 1.1 gather.31
  404.0 6.4 %gather_fusion.2 = f32[2048,128]{1,0:T(8,128)S(1)} fusion(f32[256,128]{1,0:T(8,128)S(1)} %bitcast.112, s32[2048]{0:T(1024)} %broadcast_clamp_fusion.2), kind=kCustom, calls=%fused_computation.2 | custom fusion | bytes 2105344 | tf_op jit(solution)/shard_map/gather | solution.py:98
  410.4 1.1 gather.32
  411.5 8.4 %gather_fusion.3 = f32[2048,128]{1,0:T(8,128)} fusion(f32[256,128]{1,0:T(8,128)S(1)} %bitcast.111, s32[2048]{0:T(1024)} %broadcast_clamp_fusion.1), kind=kCustom, calls=%fused_computation.3 | custom fusion | bytes 2105344 | tf_op jit(solution)/shard_map/gather | solution.py:98
  420.0 2.3 gather.33
  422.3 7.6 %gather_fusion.4 = f32[2048,128]{1,0:T(8,128)} fusion(f32[256,128]{1,0:T(8,128)S(1)} %bitcast.110, s32[2048]{0:T(1024)S(1)} %copy-done.44), kind=kCustom, calls=%fused_computation.4 | custom fusion | bytes 2105344 | tf_op jit(solution)/shard_map/gather | solution.py:98
  430.0 2.4 gather.34
  432.4 3.5 subtract_convert_fusion
  438.6 1.9 dynamic-slice_subtract_fusion
  443.6 2.3 clamp_subtract_fusion
  (154 shorter events, 20.0 us)
Async XLA Ops:
  7.2 168.6 %reduce-scatter.2.cloned.1.call-start = ((), (), s32[]{:S(2)}) async-start(), calls=%async_computation.2 | async-start | bytes 17825792 | tf_op jit(solution)/shard_map/reduce_scatter | solution.py:60
  19.2 246.4 %all-gather.3.cloned.1.call-start = ((), (), s32[]{:S(2)}) async-start(), calls=%async_computation.1 | async-start | bytes 8912896 | tf_op jit(solution)/shard_map/all_gather | solution.py:56
  19.9 360.0 %all-gather.5.cloned.1.call-start = ((), (), s32[]{:S(2)}) async-start(), calls=%async_computation.3 | async-start | bytes 11141120 | tf_op jit(solution)/shard_map/all_gather | solution.py:86
  20.1 157.6 %copy-start.29 = (bf16[2048]{0:T(1024)(128)(2,1)}, bf16[2048]{0:T(1024)(128)(2,1)S(1)}, u32[]{:S(2)}) copy-start(bf16[2048]{0:T(1024)(128)(2,1)S(1)} %get-tuple-element.13) | copy-start | bytes 12292
  20.1 159.8 %copy-start.31 = (bf16[2048]{0:T(1024)(128)(2,1)}, bf16[2048]{0:T(1024)(128)(2,1)S(1)}, u32[]{:S(2)}) copy-start(bf16[2048]{0:T(1024)(128)(2,1)S(1)} %get-tuple-element.12) | copy-start | bytes 12292
  20.1 160.2 %copy-start.33 = (bf16[2048]{0:T(1024)(128)(2,1)}, bf16[2048]{0:T(1024)(128)(2,1)S(1)}, u32[]{:S(2)}) copy-start(bf16[2048]{0:T(1024)(128)(2,1)S(1)} %get-tuple-element.11) | copy-start | bytes 12292
  20.2 160.7 %copy-start.35 = (bf16[2048]{0:T(1024)(128)(2,1)}, bf16[2048]{0:T(1024)(128)(2,1)S(1)}, u32[]{:S(2)}) copy-start(bf16[2048]{0:T(1024)(128)(2,1)S(1)} %get-tuple-element.10) | copy-start | bytes 12292
  20.2 161.1 %copy-start.37 = (bf16[2048]{0:T(1024)(128)(2,1)}, bf16[2048]{0:T(1024)(128)(2,1)S(1)}, u32[]{:S(2)}) copy-start(bf16[2048]{0:T(1024)(128)(2,1)S(1)} %get-tuple-element.9) | copy-start | bytes 12292
  20.2 160.2 %copy-start.19 = (s32[1,2048]{1,0:T(1,128)}, s32[1,2048]{1,0:T(1,128)S(1)}, u32[]{:S(2)}) copy-start(s32[1,2048]{1,0:T(1,128)S(1)} %get-tuple-element.38) | copy-start | bytes 24580
  20.2 160.6 %copy-start.21 = (s32[1,2048]{1,0:T(1,128)}, s32[1,2048]{1,0:T(1,128)S(1)}, u32[]{:S(2)}) copy-start(s32[1,2048]{1,0:T(1,128)S(1)} %get-tuple-element.41) | copy-start | bytes 24580
  20.2 161.1 %copy-start.23 = (s32[1,2048]{1,0:T(1,128)}, s32[1,2048]{1,0:T(1,128)S(1)}, u32[]{:S(2)}) copy-start(s32[1,2048]{1,0:T(1,128)S(1)} %get-tuple-element.37) | copy-start | bytes 24580
  180.8 9.8 %copy-start.27 = (f32[1,5,2048]{2,0,1:T(1,128)S(1)}, f32[1,5,2048]{2,0,1:T(1,128)}, u32[]{:S(2)}) copy-start(f32[1,5,2048]{2,0,1:T(1,128)} %param.14) | copy-start | bytes 122884
  180.8 48.9 %copy-start.28 = (f32[1,5,2048]{2,0,1:T(1,128)S(1)}, f32[1,5,2048]{2,0,1:T(1,128)}, u32[]{:S(2)}) copy-start(f32[1,5,2048]{2,0,1:T(1,128)} %param.15) | copy-start | bytes 122884
  181.3 84.2 %copy-start.2 = (bf16[128,8192]{1,0:T(8,128)(2,1)S(1)}, bf16[128,8192]{1,0:T(8,128)(2,1)}, u32[]{:S(2)}) copy-start(bf16[128,8192]{1,0:T(8,128)(2,1)} %param.8) | copy-start | bytes 6291460
  181.3 84.2 %copy-start.17 = (f32[8192]{0:T(1024)S(1)}, f32[8192]{0:T(1024)}, u32[]{:S(2)}) copy-start(f32[8192]{0:T(1024)} %param.9) | copy-start | bytes 98308
  274.1 114.3 %copy-start.9 = (f32[1,5,32768]{2,0,1:T(1,128)S(1)}, f32[1,5,32768]{2,0,1:T(1,128)}, u32[]{:S(2)}) copy-start(f32[1,5,32768]{2,0,1:T(1,128)} %all_gather.13) | copy-start | bytes 1966084
  274.1 114.3 %copy-start.10 = (f32[1,5,32768]{2,0,1:T(1,128)S(1)}, f32[1,5,32768]{2,0,1:T(1,128)}, u32[]{:S(2)}) copy-start(f32[1,5,32768]{2,0,1:T(1,128)} %all_gather.15) | copy-start | bytes 1966084
  411.5 10.8 %copy-start.44 = (s32[2048]{0:T(1024)S(1)}, s32[2048]{0:T(1024)}, u32[]{:S(2)}) copy-start(s32[2048]{0:T(1024)} %broadcast_clamp_fusion) | copy-start | bytes 24580
  422.3 10.1 %copy-start.39 = (f32[1,2048]{1,0:T(1,128)S(1)}, f32[1,2048]{1,0:T(1,128)}, u32[]{:S(2)}) copy-start(f32[1,2048]{1,0:T(1,128)} %get-tuple-element.25) | copy-start | bytes 24580
  422.3 10.1 %copy-start.40 = (f32[1,2048]{1,0:T(1,128)S(1)}, f32[1,2048]{1,0:T(1,128)}, u32[]{:S(2)}) copy-start(f32[1,2048]{1,0:T(1,128)} %get-tuple-element.26) | copy-start | bytes 24580
  422.3 10.1 %copy-start.41 = (f32[1,2048]{1,0:T(1,128)S(1)}, f32[1,2048]{1,0:T(1,128)}, u32[]{:S(2)}) copy-start(f32[1,2048]{1,0:T(1,128)} %get-tuple-element.27) | copy-start | bytes 24580
  422.3 10.1 %copy-start.42 = (f32[1,2048]{1,0:T(1,128)S(1)}, f32[1,2048]{1,0:T(1,128)}, u32[]{:S(2)}) copy-start(f32[1,2048]{1,0:T(1,128)} %get-tuple-element.28) | copy-start | bytes 24580
  422.3 10.1 %copy-start.43 = (f32[1,2048]{1,0:T(1,128)S(1)}, f32[1,2048]{1,0:T(1,128)}, u32[]{:S(2)}) copy-start(f32[1,2048]{1,0:T(1,128)} %get-tuple-element.29) | copy-start | bytes 24580
  430.0 6.3 %copy-start.22 = (s32[1,2048]{1,0:T(1,128)S(1)}, s32[1,2048]{1,0:T(1,128)}, u32[]{:S(2)}) copy-start(s32[1,2048]{1,0:T(1,128)} %copy-done.21) | copy-start | bytes 24580
  (24 other events, 109.9 us)
Sparse Core Ops, SparseCore 0:
  19.3 156.4 reduce-scatter.1
  178.5 80.8 all-gather.2
  261.7 118.1 all-gather.4
